TPU v7x, 32 devices: a 4x4x1 block of a 4x4x8 slice. The times are simulated.
32 devices in a mesh: batch: 1 (over z), ysp: 4 (over y), xsp: 8 (over x, core).
Axes of the slice: x: 4, y: 4, z: 1, core: 2. Of those that a mesh axis runs over, the one named last changes fastest.
The devices are a block of a 4x4x8 slice.
Arguments:
- volume: bfloat16 [64, 256, 128, 128], P('batch', 'xsp', 'ysp')
- filter_taps: float32 [3, 3, 21], replicated
- mix_weights: bfloat16 [3, 64, 64], replicated
- mix_bias: float32 [3, 64], replicated
Outputs:
- output: bfloat16 [64, 256, 128, 128], P('batch', 'xsp', 'ysp')
All inputs are finite; a program needn't handle non-finite values.
Results may differ from a plain program's by a relative error of at most 0.00648.
Values are sent between devices in bfloat16 or wider.
A program may use at most 768 MiB of HBM per device.

v0:
```python
import jax
import jax.numpy as jnp
from jax import lax
from jax.sharding import PartitionSpec as P

PARTS_AXIS = "batch"
COL_AXIS = "ysp"
ROW_AXIS = "xsp"
DEPTH_TILE = 128


def band_matrix(tap_row, n_rows, n_cols, offset):
    tap_count = tap_row.shape[0]
    tap_index = jnp.arange(n_rows)[:, None] - jnp.arange(n_cols)[None, :] + offset
    tap_vals = tap_row.astype(jnp.bfloat16)[jnp.clip(tap_index, 0, tap_count - 1)]
    in_band = (tap_index >= 0) & (tap_index < tap_count)
    return jnp.where(in_band, tap_vals, jnp.zeros_like(tap_vals))


def depth_pass(operand, tap_row):
    half_width = (tap_row.shape[0] - 1) // 2
    depth_len = operand.shape[3]
    tile_len = min(DEPTH_TILE, depth_len)
    n_tiles = depth_len // tile_len
    tiled_op = operand.reshape(operand.shape[:3] + (n_tiles, tile_len))
    same_band = band_matrix(tap_row, tile_len, tile_len, half_width)
    if n_tiles == 1:
        filtered = jnp.einsum("cxyqa,ai->cxyqi", tiled_op, same_band, preferred_element_type=jnp.float32)
    else:
        band_cat = jnp.concatenate([same_band, band_matrix(tap_row, tile_len, tile_len, half_width - tile_len), band_matrix(tap_row, tile_len, tile_len, half_width + tile_len)], axis=1)
        spread = jnp.einsum("cxyqa,ai->cxyqi", tiled_op, band_cat, preferred_element_type=jnp.float32)
        own_tile = spread[..., :tile_len]
        to_next = spread[..., tile_len:2 * tile_len]
        to_prev = spread[..., 2 * tile_len:]
        zero_tile = jnp.zeros_like(own_tile[:, :, :, :1])
        filtered = own_tile + jnp.concatenate([zero_tile, to_next[:, :, :, :-1]], axis=3) + jnp.concatenate([to_prev[:, :, :, 1:], zero_tile], axis=3)
    return filtered.reshape(operand.shape).astype(jnp.bfloat16)


def halo_pass(operand, tap_row, dim_index, axis_name, axis_size, eq_form):
    half_width = (tap_row.shape[0] - 1) // 2
    extent = operand.shape[dim_index]
    tail_planes = lax.slice_in_dim(operand, extent - half_width, extent, axis=dim_index)
    head_planes = lax.slice_in_dim(operand, 0, half_width, axis=dim_index)
    if axis_size > 1:
        from_left = lax.ppermute(tail_planes, axis_name, [(source, source + 1) for source in range(axis_size - 1)])
        from_right = lax.ppermute(head_planes, axis_name, [(source + 1, source) for source in range(axis_size - 1)])
    else:
        from_left = jnp.zeros_like(tail_planes)
        from_right = jnp.zeros_like(head_planes)
    padded = jnp.concatenate([from_left, operand, from_right], axis=dim_index)
    toeplitz = band_matrix(tap_row, extent + 2 * half_width, extent, 0)
    return jnp.einsum(eq_form, padded, toeplitz, preferred_element_type=jnp.float32).astype(jnp.bfloat16)


def mix_residual(current, filtered, mix_mat, bias_vec):
    pre_act = jnp.einsum("cd,cxyz->dxyz", mix_mat, filtered, preferred_element_type=jnp.float32) + bias_vec[:, None, None, None]
    return (current.astype(jnp.float32) + jax.nn.gelu(pre_act, approximate=True)).astype(jnp.bfloat16)


def solution(mesh):
    x_count = mesh.shape[ROW_AXIS]
    y_count = mesh.shape[COL_AXIS]
    vol_spec = P(PARTS_AXIS, ROW_AXIS, COL_AXIS, None)

    def local_layers(volume, filter_taps, mix_weights, mix_bias):
        current = volume
        for layer_idx in range(filter_taps.shape[0]):
            x_filtered = halo_pass(current, filter_taps[layer_idx, 0], 1, ROW_AXIS, x_count, "cayz,ai->ciyz")
            xy_filtered = halo_pass(x_filtered, filter_taps[layer_idx, 1], 2, COL_AXIS, y_count, "cxaz,ai->cxiz")
            xyz_filtered = depth_pass(xy_filtered, filter_taps[layer_idx, 2])
            current = mix_residual(current, xyz_filtered, mix_weights[layer_idx], mix_bias[layer_idx])
        return current

    return jax.shard_map(local_layers, mesh=mesh, in_specs=(vol_spec, P(), P(), P()), out_specs=vol_spec, check_vma=False)
```

profile of v0, /device:TPU:122, one launch (start us, length us, event | category | flops | bytes accessed | tf_op | source)
XLA Modules:
  0.0 1143.5 jit_solution(13341754102947978111)
XLA Ops:
  0.0 10.0 fusion.533
  10.0 1.9 collective-permute-start.1
  12.0 2.4 collective-permute-start
  14.4 17.5 %copy.30 = bf16[64,32,32,128]{3,1,2,0:T(8,128)(2,1)} copy(bf16[64,32,32,128]{3,2,1,0:T(8,128)(2,1)} %param.4) | data formatting | bytes 33554432 | tf_op args[0]
  32.0 0.6 slice_bitcast_fusion.1
  32.6 10.0 gather_fusion.1
  42.7 0.1 reshape.101
  42.7 26.4 %collective-permute-done.1 = bf16[64,10,32,128]{3,2,1,0:T(8,128)(2,1)} collective-permute-done((bf16[64,10,32,128]{3,2,1,0:T(8,128)(2,1)}, bf16[64,10,32,128]{3,2,1,0:T(8,128)(2,1)}, u32[]{:S(2)}, u32[]{:S(2)}) %collective-permute-start.1) | collective-permute-done | bytes 5242912 | tf_op jit(solution)/shard_map/ppermute | solution.py:47
  69.2 11.1 copy.31
  80.2 11.0 copy.29
  91.2 24.5 %convert_bitcast_fusion.5 = bf16[64,32,32,128]{3,1,2,0:T(8,128)(2,1)} fusion(bf16[64,10,32,128]{3,1,2,0:T(8,128)(2,1)} %copy.31, bf16[64,32,32,128]{3,1,2,0:T(8,128)(2,1)} %copy.30, bf16[64,10,32,128]{3,1,2,0:T(8,128)(2,1)} %copy.29, bf16[52,32]{1,0:T(8,128)(2,1)S(1)} %reshape.101), kind=kOutput, calls=%fused_computation.74 | convolution fusion | flops 962601088 | bytes 44043520 | tf_op jit(solution)/shard_map/cayz,ai->ciyz/dot_general | solution.py:53
  115.8 10.2 fusion.532
  125.9 4.4 collective-permute-start.3
  130.4 1.3 collective-permute-start.2
  131.7 9.7 gather_fusion
  141.4 0.1 reshape.93
  141.5 0.7 fusion.537
  142.2 0.7 fusion.536
  142.9 0.5 slice_bitcast_fusion.6
  143.5 96.7 %collective-permute-done.3 = bf16[64,32,10,128]{3,1,2,0:T(8,128)(2,1)} collective-permute-done((bf16[64,32,10,128]{3,1,2,0:T(8,128)(2,1)}, bf16[64,32,10,128]{3,1,2,0:T(8,128)(2,1)}, u32[]{:S(2)}, u32[]{:S(2)}) %collective-permute-start.3) | collective-permute-done | bytes 5242912 | tf_op jit(solution)/shard_map/ppermute | solution.py:47
  240.1 7.0 collective-permute-done.2
  247.2 18.8 %pad_maximum_fusion = bf16[64,32,52,128]{3,1,2,0:T(8,128)(2,1)} fusion(bf16[64,32,10,128]{3,1,2,0:T(8,128)(2,1)} %collective-permute-done.3, bf16[64,32,32,128]{3,1,2,0:T(8,128)(2,1)} %convert_bitcast_fusion.5, bf16[64,32,10,128]{3,1,2,0:T(8,128)(2,1)} %collective-permute-done.2), kind=kLoop, calls=%fused_computation.52 | loop fusion | flops 27262976 | bytes 54525952 | tf_op jit(solution)/shard_map/concatenate | solution.py:51
  266.0 28.6 %convert_bitcast_fusion.4 = bf16[64,32,32,128]{3,2,1,0:T(8,128)(2,1)} fusion(bf16[64,32,52,128]{3,1,2,0:T(8,128)(2,1)} %pad_maximum_fusion, bf16[52,32]{1,0:T(8,128)(2,1)S(1)} %reshape.93), kind=kOutput, calls=%fused_computation.73 | convolution fusion | flops 880812160 | bytes 44043520 | tf_op jit(solution)/shard_map/cxaz,ai->cxiz/dot_general | solution.py:53
  294.6 54.6 %fusion.8 = bf16[64,32,32,128]{3,0,2,1:T(8,128)(2,1)} fusion(bf16[64,32,32,128]{3,2,1,0:T(8,128)(2,1)} %param.4, f32[64]{0:T(128)S(1)} %get-tuple-element.87, bf16[64,32,32,128]{3,2,1,0:T(8,128)(2,1)} %convert_bitcast_fusion.4, bf16[]{:T(256)} %bitcast.34, bf16[]{:T(256)} %bitcast.35, bf16[]{:T(256)} %bitcast.36, bf16[]{:T(256)} %bitcast.37, bf16[]{:T(256)} %bitcast.38, ...), kind=kOutput, calls=%fused_computation.17 | convolution fusion | flops 3331129344 | bytes 50348584 | tf_op jit(solution)/shard_map/cd,cxyz->dxyz/dot_general | solution.py:57
  349.1 11.7 %fusion.531 = (bf16[64,10,32,128]{3,0,2,1:T(8,128)(2,1)}, bf16[64,10,32,128]{3,0,2,1:T(8,128)(2,1)}) fusion(bf16[64,32,32,128]{3,0,2,1:T(8,128)(2,1)} %fusion.8), kind=kLoop, calls=%fused_computation.355 | loop fusion | bytes 20971520 | tf_op jit(solution)/shard_map/slice | solution.py:43
  360.8 1.9 collective-permute-start.5
  362.8 2.8 collective-permute-start.4
  365.6 9.7 gather_fusion.3
  375.4 0.1 reshape.145
  375.5 44.5 %collective-permute-done.5 = bf16[64,10,32,128]{3,0,2,1:T(8,128)(2,1)} collective-permute-done((bf16[64,10,32,128]{3,0,2,1:T(8,128)(2,1)}, bf16[64,10,32,128]{3,0,2,1:T(8,128)(2,1)}, u32[]{:S(2)}, u32[]{:S(2)}) %collective-permute-start.5) | collective-permute-done | bytes 5242912 | tf_op jit(solution)/shard_map/ppermute | solution.py:47
  420.0 3.9 collective-permute-done.4
  423.9 18.9 %pad_maximum_fusion.1 = bf16[64,52,32,128]{3,0,2,1:T(8,128)(2,1)} fusion(bf16[64,10,32,128]{3,0,2,1:T(8,128)(2,1)} %collective-permute-done.5, bf16[64,32,32,128]{3,0,2,1:T(8,128)(2,1)} %fusion.8, bf16[64,10,32,128]{3,0,2,1:T(8,128)(2,1)} %collective-permute-done.4), kind=kLoop, calls=%fused_computation.53 | loop fusion | flops 27262976 | bytes 54525952 | tf_op jit(solution)/shard_map/concatenate | solution.py:51
  442.8 69.1 %convert_bitcast_fusion.3 = bf16[64,32,32,128]{3,1,2,0:T(8,128)(2,1)} fusion(bf16[64,52,32,128]{3,0,2,1:T(8,128)(2,1)} %pad_maximum_fusion.1, bf16[52,32]{1,0:T(8,128)(2,1)S(1)} %reshape.145), kind=kOutput, calls=%fused_computation.70 | convolution fusion | flops 880812160 | bytes 44043520 | tf_op jit(solution)/shard_map/cayz,ai->ciyz/dot_general | solution.py:53
  511.9 10.1 fusion.530
  522.0 3.8 collective-permute-start.7
  525.7 1.3 collective-permute-start.6
  527.0 9.7 gather_fusion.2
  536.8 0.1 reshape.137
  536.9 0.7 fusion.535
  537.6 0.7 fusion.534
  538.4 97.9 %collective-permute-done.7 = bf16[64,32,10,128]{3,1,2,0:T(8,128)(2,1)} collective-permute-done((bf16[64,32,10,128]{3,1,2,0:T(8,128)(2,1)}, bf16[64,32,10,128]{3,1,2,0:T(8,128)(2,1)}, u32[]{:S(2)}, u32[]{:S(2)}) %collective-permute-start.7) | collective-permute-done | bytes 5242912 | tf_op jit(solution)/shard_map/ppermute | solution.py:47
  636.3 6.5 collective-permute-done.6
  642.7 18.8 %pad_maximum_fusion.2 = bf16[64,32,52,128]{3,1,2,0:T(8,128)(2,1)} fusion(bf16[64,32,10,128]{3,1,2,0:T(8,128)(2,1)} %collective-permute-done.7, bf16[64,32,32,128]{3,1,2,0:T(8,128)(2,1)} %convert_bitcast_fusion.3, bf16[64,32,10,128]{3,1,2,0:T(8,128)(2,1)} %collective-permute-done.6), kind=kLoop, calls=%fused_computation.54 | loop fusion | flops 27262976 | bytes 54525952 | tf_op jit(solution)/shard_map/concatenate | solution.py:51
  661.6 28.6 %convert_bitcast_fusion.2 = bf16[64,32,32,128]{3,2,1,0:T(8,128)(2,1)} fusion(bf16[64,32,52,128]{3,1,2,0:T(8,128)(2,1)} %pad_maximum_fusion.2, bf16[52,32]{1,0:T(8,128)(2,1)S(1)} %reshape.137), kind=kOutput, calls=%fused_computation.69 | convolution fusion | flops 880812160 | bytes 44043520 | tf_op jit(solution)/shard_map/cxaz,ai->cxiz/dot_general | solution.py:53
  690.1 49.3 %fusion.17 = bf16[64,32,32,128]{3,0,2,1:T(8,128)(2,1)} fusion(bf16[64,32,32,128]{3,0,2,1:T(8,128)(2,1)} %fusion.8, f32[64]{0:T(128)S(1)} %get-tuple-element.88, bf16[64,32,32,128]{3,2,1,0:T(8,128)(2,1)} %convert_bitcast_fusion.2, bf16[]{:T(256)} %bitcast.69, bf16[]{:T(256)} %bitcast.70, bf16[]{:T(256)} %bitcast.71, bf16[]{:T(256)} %bitcast.72, ...), kind=kOutput, calls=%fused_computation.26 | convolution fusion | flops 3331129344 | bytes 50348584 | tf_op jit(solution)/shard_map/cd,cxyz->dxyz/dot_general | solution.py:57
  739.5 11.7 %fusion.529 = (bf16[64,10,32,128]{3,0,2,1:T(8,128)(2,1)}, bf16[64,10,32,128]{3,0,2,1:T(8,128)(2,1)}) fusion(bf16[64,32,32,128]{3,0,2,1:T(8,128)(2,1)} %fusion.17), kind=kLoop, calls=%fused_computation.353 | loop fusion | bytes 20971520 | tf_op jit(solution)/shard_map/slice | solution.py:43
  751.2 1.9 collective-permute-start.9
  753.1 2.4 collective-permute-start.8
  755.6 9.7 gather_fusion.5
  765.4 44.9 %collective-permute-done.9 = bf16[64,10,32,128]{3,0,2,1:T(8,128)(2,1)} collective-permute-done((bf16[64,10,32,128]{3,0,2,1:T(8,128)(2,1)}, bf16[64,10,32,128]{3,0,2,1:T(8,128)(2,1)}, u32[]{:S(2)}, u32[]{:S(2)}) %collective-permute-start.9) | collective-permute-done | bytes 5242912 | tf_op jit(solution)/shard_map/ppermute | solution.py:47
  810.3 3.9 collective-permute-done.8
  814.2 18.9 %pad_maximum_fusion.3 = bf16[64,52,32,128]{3,0,2,1:T(8,128)(2,1)} fusion(bf16[64,10,32,128]{3,0,2,1:T(8,128)(2,1)} %collective-permute-done.9, bf16[64,32,32,128]{3,0,2,1:T(8,128)(2,1)} %fusion.17, bf16[64,10,32,128]{3,0,2,1:T(8,128)(2,1)} %collective-permute-done.8), kind=kLoop, calls=%fused_computation.55 | loop fusion | flops 27262976 | bytes 54525952 | tf_op jit(solution)/shard_map/concatenate | solution.py:51
  833.1 69.1 %convert_bitcast_fusion.1 = bf16[64,32,32,128]{3,1,2,0:T(8,128)(2,1)} fusion(bf16[64,52,32,128]{3,0,2,1:T(8,128)(2,1)} %pad_maximum_fusion.3, bf16[52,32]{1,0:T(8,128)(2,1)S(1)} %reshape.189), kind=kOutput, calls=%fused_computation.66 | convolution fusion | flops 880812160 | bytes 44043520 | tf_op jit(solution)/shard_map/cayz,ai->ciyz/dot_general | solution.py:53
  902.2 10.1 fusion.528
  912.3 3.8 collective-permute-start.11
  916.1 1.3 collective-permute-start.10
  917.4 9.7 gather_fusion.4
  927.1 0.1 reshape.181
  927.2 98.3 %collective-permute-done.11 = bf16[64,32,10,128]{3,1,2,0:T(8,128)(2,1)} collective-permute-done((bf16[64,32,10,128]{3,1,2,0:T(8,128)(2,1)}, bf16[64,32,10,128]{3,1,2,0:T(8,128)(2,1)}, u32[]{:S(2)}, u32[]{:S(2)}) %collective-permute-start.11) | collective-permute-done | bytes 5242912 | tf_op jit(solution)/shard_map/ppermute | solution.py:47
  1025.6 6.5 collective-permute-done.10
  1032.0 18.8 %pad_maximum_fusion.4 = bf16[64,32,52,128]{3,1,2,0:T(8,128)(2,1)} fusion(bf16[64,32,10,128]{3,1,2,0:T(8,128)(2,1)} %collective-permute-done.11, bf16[64,32,32,128]{3,1,2,0:T(8,128)(2,1)} %convert_bitcast_fusion.1, bf16[64,32,10,128]{3,1,2,0:T(8,128)(2,1)} %collective-permute-done.10), kind=kLoop, calls=%fused_computation.56 | loop fusion | flops 27262976 | bytes 54525952 | tf_op jit(solution)/shard_map/concatenate | solution.py:51
  1050.9 28.6 %convert_bitcast_fusion = bf16[64,32,32,128]{3,2,1,0:T(8,128)(2,1)} fusion(bf16[64,32,52,128]{3,1,2,0:T(8,128)(2,1)} %pad_maximum_fusion.4, bf16[52,32]{1,0:T(8,128)(2,1)S(1)} %reshape.181), kind=kOutput, calls=%fused_computation.65 | convolution fusion | flops 880812160 | bytes 44043520 | tf_op jit(solution)/shard_map/cxaz,ai->cxiz/dot_general | solution.py:53
  1079.4 48.7 %fusion.26 = bf16[64,32,32,128]{3,0,2,1:T(8,128)(2,1)} fusion(bf16[64,32,32,128]{3,0,2,1:T(8,128)(2,1)} %fusion.17, f32[64]{0:T(128)S(1)} %copy-done.4, bf16[64,32,32,128]{3,2,1,0:T(8,128)(2,1)} %convert_bitcast_fusion, bf16[]{:T(256)} %bitcast.104, bf16[]{:T(256)} %bitcast.105, bf16[]{:T(256)} %bitcast.106, bf16[]{:T(256)} %bitcast.107, bf16[]{:T(256)} %bitcast.108, ...), kind=kOutput, calls=%fused_computation.35 | convolution fusion | flops 3331129344 | bytes 50348584 | tf_op jit(solution)/shard_map/cd,cxyz->dxyz/dot_general | solution.py:57
  1128.2 15.2 %copy.49 = bf16[64,32,32,128]{3,2,1,0:T(8,128)(2,1)} copy(bf16[64,32,32,128]{3,0,2,1:T(8,128)(2,1)} %fusion.26) | data formatting | bytes 33554432 | tf_op jit(solution)/shard_map/convert_element_type | solution.py:58
  (18 shorter events, 0.2 us)
Async XLA Ops:
  0.0 31.9 %copy-start.2 = (f32[3,3,21]{2,1,0:T(4,128)S(1)}, f32[3,3,21]{2,1,0:T(4,128)}, u32[]{:S(2)}) copy-start(f32[3,3,21]{2,1,0:T(4,128)} %param.5) | copy-start | bytes 2272
  10.0 59.2 %collective-permute-start.1 = (bf16[64,10,32,128]{3,2,1,0:T(8,128)(2,1)}, bf16[64,10,32,128]{3,2,1,0:T(8,128)(2,1)}, u32[]{:S(2)}, u32[]{:S(2)}) collective-permute-start(bf16[64,10,32,128]{3,2,1,0:T(8,128)(2,1)} %get-tuple-element.16), channel_id=1, source_target_pairs={{1,0},{2,1},{3,2},{4,3},{5,4},{6,5},{7,6},{9,8},{10,9},{11,10},{12... | collective-permute-start | bytes 15728648 | tf_op jit(solution)/shard_map/ppermute | solution.py:47
  12.0 68.3 %collective-permute-start = (bf16[64,10,32,128]{3,2,1,0:T(8,128)(2,1)}, bf16[64,10,32,128]{3,2,1,0:T(8,128)(2,1)}, u32[]{:S(2)}, u32[]{:S(2)}) collective-permute-start(bf16[64,10,32,128]{3,2,1,0:T(8,128)(2,1)} %get-tuple-element.15), channel_id=1, source_target_pairs={{0,1},{1,2},{2,3},{3,4},{4,5},{5,6},{6,7},{8,9},{9,10},{10,11},{11... | collective-permute-start | bytes 15728648 | tf_op jit(solution)/shard_map/ppermute | solution.py:46
  115.8 27.1 %copy-start.3 = (f32[3,64]{1,0:T(4,128)S(1)}, f32[3,64]{1,0:T(4,128)}, u32[]{:S(2)}) copy-start(f32[3,64]{1,0:T(4,128)} %param.7) | copy-start | bytes 2308
  125.9 114.2 %collective-permute-start.3 = (bf16[64,32,10,128]{3,1,2,0:T(8,128)(2,1)}, bf16[64,32,10,128]{3,1,2,0:T(8,128)(2,1)}, u32[]{:S(2)}, u32[]{:S(2)}) collective-permute-start(bf16[64,32,10,128]{3,1,2,0:T(8,128)(2,1)} %get-tuple-element.14), channel_id=1, source_target_pairs={{8,0},{16,8},{24,16},{9,1},{17,9},{25,17},{10,2},{18,10},{26,18},{... | collective-permute-start | bytes 15728648 | tf_op jit(solution)/shard_map/ppermute | solution.py:47
  130.4 116.8 %collective-permute-start.2 = (bf16[64,32,10,128]{3,1,2,0:T(8,128)(2,1)}, bf16[64,32,10,128]{3,1,2,0:T(8,128)(2,1)}, u32[]{:S(2)}, u32[]{:S(2)}) collective-permute-start(bf16[64,32,10,128]{3,1,2,0:T(8,128)(2,1)} %get-tuple-element.13), channel_id=1, source_target_pairs={{0,8},{8,16},{16,24},{1,9},{9,17},{17,25},{2,10},{10,18},{18,26},{... | collective-permute-start | bytes 15728648 | tf_op jit(solution)/shard_map/ppermute | solution.py:46
  266.0 28.6 %copy-start.5 = (bf16[3,64,64]{2,1,0:T(8,128)(2,1)S(1)}, bf16[3,64,64]{2,1,0:T(8,128)(2,1)}, u32[]{:S(2)}) copy-start(bf16[3,64,64]{2,1,0:T(8,128)(2,1)} %param.6) | copy-start | bytes 73732
  360.8 59.2 %collective-permute-start.5 = (bf16[64,10,32,128]{3,0,2,1:T(8,128)(2,1)}, bf16[64,10,32,128]{3,0,2,1:T(8,128)(2,1)}, u32[]{:S(2)}, u32[]{:S(2)}) collective-permute-start(bf16[64,10,32,128]{3,0,2,1:T(8,128)(2,1)} %get-tuple-element.12), channel_id=1, source_target_pairs={{1,0},{2,1},{3,2},{4,3},{5,4},{6,5},{7,6},{9,8},{10,9},{11,10},{12... | collective-permute-start | bytes 15728648 | tf_op jit(solution)/shard_map/ppermute | solution.py:47
  362.8 61.1 %collective-permute-start.4 = (bf16[64,10,32,128]{3,0,2,1:T(8,128)(2,1)}, bf16[64,10,32,128]{3,0,2,1:T(8,128)(2,1)}, u32[]{:S(2)}, u32[]{:S(2)}) collective-permute-start(bf16[64,10,32,128]{3,0,2,1:T(8,128)(2,1)} %get-tuple-element.11), channel_id=1, source_target_pairs={{0,1},{1,2},{2,3},{3,4},{4,5},{5,6},{6,7},{8,9},{9,10},{10,11},{11... | collective-permute-start | bytes 15728648 | tf_op jit(solution)/shard_map/ppermute | solution.py:46
  522.0 114.3 %collective-permute-start.7 = (bf16[64,32,10,128]{3,1,2,0:T(8,128)(2,1)}, bf16[64,32,10,128]{3,1,2,0:T(8,128)(2,1)}, u32[]{:S(2)}, u32[]{:S(2)}) collective-permute-start(bf16[64,32,10,128]{3,1,2,0:T(8,128)(2,1)} %get-tuple-element.10), channel_id=1, source_target_pairs={{8,0},{16,8},{24,16},{9,1},{17,9},{25,17},{10,2},{18,10},{26,18},{... | collective-permute-start | bytes 15728648 | tf_op jit(solution)/shard_map/ppermute | solution.py:47
  525.7 117.0 %collective-permute-start.6 = (bf16[64,32,10,128]{3,1,2,0:T(8,128)(2,1)}, bf16[64,32,10,128]{3,1,2,0:T(8,128)(2,1)}, u32[]{:S(2)}, u32[]{:S(2)}) collective-permute-start(bf16[64,32,10,128]{3,1,2,0:T(8,128)(2,1)} %get-tuple-element.9), channel_id=1, source_target_pairs={{0,8},{8,16},{16,24},{1,9},{9,17},{17,25},{2,10},{10,18},{18,26},{... | collective-permute-start | bytes 15728648 | tf_op jit(solution)/shard_map/ppermute | solution.py:46
  739.5 16.1 %copy-start.1 = (bf16[21]{0:T(256)(128)(2,1)S(1)}, bf16[21]{0:T(256)(128)(2,1)}, u32[]{:S(2)}) copy-start(bf16[21]{0:T(256)(128)(2,1)} %get-tuple-element.81) | copy-start | bytes 130
  751.2 59.2 %collective-permute-start.9 = (bf16[64,10,32,128]{3,0,2,1:T(8,128)(2,1)}, bf16[64,10,32,128]{3,0,2,1:T(8,128)(2,1)}, u32[]{:S(2)}, u32[]{:S(2)}) collective-permute-start(bf16[64,10,32,128]{3,0,2,1:T(8,128)(2,1)} %get-tuple-element.8), channel_id=1, source_target_pairs={{1,0},{2,1},{3,2},{4,3},{5,4},{6,5},{7,6},{9,8},{10,9},{11,10},{12... | collective-permute-start | bytes 15728648 | tf_op jit(solution)/shard_map/ppermute | solution.py:47
  753.1 61.1 %collective-permute-start.8 = (bf16[64,10,32,128]{3,0,2,1:T(8,128)(2,1)}, bf16[64,10,32,128]{3,0,2,1:T(8,128)(2,1)}, u32[]{:S(2)}, u32[]{:S(2)}) collective-permute-start(bf16[64,10,32,128]{3,0,2,1:T(8,128)(2,1)} %get-tuple-element.7), channel_id=1, source_target_pairs={{0,1},{1,2},{2,3},{3,4},{4,5},{5,6},{6,7},{8,9},{9,10},{10,11},{11... | collective-permute-start | bytes 15728648 | tf_op jit(solution)/shard_map/ppermute | solution.py:46
  833.1 84.3 %copy-start = (bf16[21]{0:T(256)(128)(2,1)S(1)}, bf16[21]{0:T(256)(128)(2,1)}, u32[]{:S(2)}) copy-start(bf16[21]{0:T(256)(128)(2,1)} %get-tuple-element.80) | copy-start | bytes 130
  912.3 113.3 %collective-permute-start.11 = (bf16[64,32,10,128]{3,1,2,0:T(8,128)(2,1)}, bf16[64,32,10,128]{3,1,2,0:T(8,128)(2,1)}, u32[]{:S(2)}, u32[]{:S(2)}) collective-permute-start(bf16[64,32,10,128]{3,1,2,0:T(8,128)(2,1)} %get-tuple-element.6), channel_id=1, source_target_pairs={{8,0},{16,8},{24,16},{9,1},{17,9},{25,17},{10,2},{18,10},{26,18},{... | collective-permute-start | bytes 15728648 | tf_op jit(solution)/shard_map/ppermute | solution.py:47
  916.1 116.0 %collective-permute-start.10 = (bf16[64,32,10,128]{3,1,2,0:T(8,128)(2,1)}, bf16[64,32,10,128]{3,1,2,0:T(8,128)(2,1)}, u32[]{:S(2)}, u32[]{:S(2)}) collective-permute-start(bf16[64,32,10,128]{3,1,2,0:T(8,128)(2,1)} %get-tuple-element.5), channel_id=1, source_target_pairs={{0,8},{8,16},{16,24},{1,9},{9,17},{17,25},{2,10},{10,18},{18,26},{... | collective-permute-start | bytes 15728648 | tf_op jit(solution)/shard_map/ppermute | solution.py:46
  1050.8 28.6 %copy-start.4 = (f32[64]{0:T(128)S(1)}, f32[64]{0:T(128)}, u32[]{:S(2)}) copy-start(f32[64]{0:T(128)} %get-tuple-element.86) | copy-start | bytes 772
where the time goes:
time: 1150 us; the launch traced here: 1140 us
  waiting for transfers between devices  437 us (38%)
  matrix products  401 us (35%)
  local copies, waits for them, and re-layouts  182 us (16%)
  other arithmetic  94.3 us (8%)
  starting transfers between devices  29.4 us (3%)
    ppermute x6, waiting for transfers between devices, halo_pass(): lax.ppermute(head_planes, axis_name, [(source + 1, source) for source in...  409 us
    dot_general x6, matrix products, halo_pass(): jnp.einsum(eq_form, padded, toeplitz, preferred_element_type=jnp.float32)  248 us
    dot_general x3, matrix products, mix_residual(): jnp.einsum('cd,cxyz->dxyz', mix_mat, filtered, preferred_element_type=jnp...  153 us
    concatenate x5, other arithmetic, halo_pass(): padded = jnp.concatenate([from_left, operand, from_right], axis=dim_index)  94.2 us
    slice x6, local copies, waits for them, and re-layouts, halo_pass(): lax.slice_in_dim(operand, extent - half_width, extent, axis=dim_index)  63.8 us
    gather x16, local copies, waits for them, and re-layouts, band_matrix(): tap_row.astype(jnp.bfloat16)[jnp.clip(tap_index, 0, tap_count - 1)]  62.1 us
    ppermute x6, waiting for transfers between devices, halo_pass(): lax.ppermute(tail_planes, axis_name, [(source, source + 1) for source in...  27.7 us
  transfers between devices with their start and end apart: 12, of which 11 were waited for; matrix products, arithmetic and copies ran while one was open for 8% of the time, Pallas kernels for 0%

commit v1 on v0

v1 whole, which is shorter than its diff:
```python
import functools

import jax
import jax.numpy as jnp
from jax import lax
from jax.experimental import pallas as pl
from jax.experimental.pallas import tpu as pltpu
from jax.sharding import PartitionSpec as P

PARTS_AXIS = "batch"
COL_AXIS = "ysp"
ROW_AXIS = "xsp"
MESH = pl.DeviceIdType.MESH
TILE = 16
CHUNK = 8
GROUPS = 4
NEAR = 2


def rows_cols(n_rows, n_cols):
    shape = (n_rows, n_cols)
    return lax.broadcasted_iota(jnp.int32, shape, 0), lax.broadcasted_iota(jnp.int32, shape, 1)


def banded(tap, n_taps, tap_index, valid):
    index = jnp.where(valid, tap_index, -1)
    total = jnp.zeros(index.shape, jnp.float32)
    for t in range(n_taps):
        total = jnp.where(index == t, tap(t), total)
    return total.astype(jnp.bfloat16)


def x_matrix(tap, n_taps, last_tile):
    half = (n_taps - 1) // 2
    own = CHUNK * TILE
    r, k = rows_cols(own + CHUNK * half, (CHUNK + 2 * half) * TILE)
    s = jnp.maximum(r - own, 0)
    plane = jnp.where(r < own, r // TILE, s // half)
    row = jnp.where(r < own, r % TILE, s % half + (TILE - half if last_tile else 0))
    return banded(tap, n_taps, k // TILE - plane, row == k % TILE)


def y_matrix(tap, n_taps, extent):
    half = (n_taps - 1) // 2
    own, slab = CHUNK * extent, CHUNK * half
    r, k = rows_cols(own, own + 2 * slab)
    s = jnp.maximum(jnp.where(k < own + slab, k - own, k - own - slab), 0)
    plane = jnp.where(k < own, k // extent, s // half)
    pos = jnp.where(k < own, k % extent + half, jnp.where(k < own + slab, s % half, s % half + half + extent))
    return banded(tap, n_taps, pos - r % extent, plane == r // extent)


def z_matrix(tap, n_taps, depth):
    r, k = rows_cols(2 * depth, 2 * depth)
    return banded(tap, n_taps, r % depth - k % depth + (n_taps - 1) // 2, r // depth == k // depth)


def mix_matrix(weight):
    n = weight.shape[0]
    r, k = rows_cols(n, n * TILE)
    across = (k // TILE == r).astype(jnp.bfloat16)
    m, c = rows_cols(n * TILE, n)
    along = (m // TILE == c).astype(jnp.bfloat16)
    wide = jnp.dot(weight.T, across, preferred_element_type=jnp.float32).astype(jnp.bfloat16)
    full = jnp.dot(along, wide, preferred_element_type=jnp.float32)
    m, k = rows_cols(n * TILE, n * TILE)
    return jnp.where(m % TILE == k % TILE, full, 0.0).astype(jnp.bfloat16)


def matrices_kernel(taps, weights, bias_col, ax0, ax1, ay, bz, wk, bias):
    n_taps = taps.shape[2]
    layer = pl.program_id(0)
    extent = ay.shape[1] // CHUNK
    ax0[0] = x_matrix(lambda t: taps[layer, 0, t], n_taps, False)
    ax1[0] = x_matrix(lambda t: taps[layer, 0, t], n_taps, True)
    ay[0] = y_matrix(lambda t: taps[layer, 1, t], n_taps, extent)
    bz[0] = z_matrix(lambda t: taps[layer, 2, t], n_taps, bz.shape[1] // 2)
    wk[0] = mix_matrix(weights[0])
    n = weights.shape[1]
    m, c = rows_cols(n * TILE, n)
    spread = jnp.sum(jnp.where(m // TILE == c, bias_col[0], 0.0), axis=1, keepdims=True)
    bias[0] = jnp.broadcast_to(spread, bias.shape[1:])


def matrices(filter_taps, mix_weights, mix_bias, extent, depth):
    layers, _, n_taps = filter_taps.shape
    chans = mix_weights.shape[1]
    half = (n_taps - 1) // 2
    taps = lax.reduce_precision(filter_taps, 8, 7)
    own_x, own_y = CHUNK * TILE, CHUNK * extent
    slab = CHUNK * half
    shapes = [(own_x + slab, own_x + 2 * half * TILE)] * 2
    shapes += [(own_y, own_y + 2 * slab), (2 * depth, 2 * depth), (chans * TILE, chans * TILE)]
    outs = [jax.ShapeDtypeStruct((layers,) + s, jnp.bfloat16) for s in shapes]
    outs.append(jax.ShapeDtypeStruct((layers, chans * TILE, depth), jnp.float32))
    return pl.pallas_call(
        matrices_kernel, grid=(layers,), out_shape=outs,
        in_specs=[pl.BlockSpec(memory_space=pltpu.SMEM), pl.BlockSpec((1, chans, chans), lambda i: (i, 0, 0)),
                  pl.BlockSpec((1, 1, chans), lambda i: (i, 0, 0))],
        out_specs=[pl.BlockSpec((1,) + o.shape[1:], lambda i: (i, 0, 0)) for o in outs],
        name="matrices",
    )(taps, mix_weights, mix_bias[:, None, :])


def gelu(v):
    c0 = 0.7978845608028654
    arg = v * (c0 + (c0 * 0.044715) * (v * v))
    h = 0.5 * v
    return h + h * jnp.tanh(arg)


def layer_kernel(layer, nx, ny, half, v_hbm, ax0_hbm, ax1_hbm, ay_hbm, bz_hbm, wk_hbm, bias_hbm, out_hbm,
                 vext, u1, send, recv, stage, ax, ay, bz, wk, bias,
                 load_sem, const_sem, xsend, xrecv, ysend, yrecv, out_sem):
    chans, planes, extent, depth = u1.shape
    n_chunks = planes // CHUNK
    per_group = chans // GROUPS
    far = half - NEAR
    slab = CHUNK * half
    window = CHUNK + 2 * half
    bi, yi, xi = lax.axis_index(PARTS_AXIS), lax.axis_index(COL_AXIS), lax.axis_index(ROW_AXIS)
    left = (bi, yi, lax.rem(xi + nx - 1, nx))
    right = (bi, yi, lax.rem(xi + 1, nx))
    up = (bi, lax.rem(yi + ny - 1, ny), xi)
    down = (bi, lax.rem(yi + 1, ny), xi)
    has_left, has_right, has_up, has_down = xi > 0, xi < nx - 1, yi > 0, yi < ny - 1

    def load(g):
        cs = pl.ds(g * per_group, per_group)
        return pltpu.make_async_copy(v_hbm.at[cs], vext.at[cs, pl.ds(half, planes)], load_sem.at[g])

    consts = [pltpu.make_async_copy(src.at[layer], dst, const_sem.at[i]) for i, (src, dst) in enumerate(
        ((ax0_hbm, ax.at[0]), (ax1_hbm, ax.at[1]), (ay_hbm, ay), (bz_hbm, bz), (wk_hbm, wk), (bias_hbm, bias)))]
    for c in consts:
        c.start()
    for g in range(GROUPS):
        load(g).start()

    barrier = pltpu.get_barrier_semaphore()
    for dev in (left, right, up, down):
        pl.semaphore_signal(barrier, inc=1, device_id=dev, device_id_type=MESH)
    pl.semaphore_wait(barrier, 4)

    def x_copy(to_right, is_far, g):
        cs = pl.ds(g * per_group, per_group)
        if to_right:
            src, dst, n = (planes - half, 0, far) if is_far else (planes - NEAR, half - NEAR, NEAR)
        else:
            src, dst, n = (NEAR, half + planes + NEAR, far) if is_far else (0, half + planes, NEAR)
        d, f = int(to_right), int(is_far)
        return pltpu.make_async_remote_copy(
            src_ref=v_hbm.at[cs, pl.ds(src, n)], dst_ref=vext.at[cs, pl.ds(dst, n)],
            send_sem=xsend.at[d, f, g], recv_sem=xrecv.at[d, f, g],
            device_id=right if to_right else left, device_id_type=MESH)

    for is_far in (False, True):
        for g in range(GROUPS):
            @pl.when(has_right)
            def _():
                x_copy(True, is_far, g).start()

            @pl.when(has_left)
            def _():
                x_copy(False, is_far, g).start()

    def fill_x(start):
        @pl.loop(0, chans)
        def _(c):
            vext[c, pl.ds(start, half)] = jnp.zeros((half, extent, depth), jnp.bfloat16)

    def fill_y(side):
        @pl.loop(0, chans)
        def _(c):
            for j in range(n_chunks):
                recv[j, side, c] = jnp.zeros((slab, depth), jnp.bfloat16)

    @pl.when(jnp.logical_not(has_left))
    def _():
        fill_x(0)

    @pl.when(jnp.logical_not(has_right))
    def _():
        fill_x(half + planes)

    @pl.when(jnp.logical_not(has_up))
    def _():
        fill_y(0)

    @pl.when(jnp.logical_not(has_down))
    def _():
        fill_y(1)

    for c in consts:
        c.wait()

    def y_copy(j, slot, side, cs):
        return pltpu.make_async_remote_copy(
            src_ref=send.at[slot, side, cs], dst_ref=recv.at[j, 1 - side, cs],
            send_sem=ysend.at[slot, side], recv_sem=yrecv.at[j, 1 - side],
            device_id=down if side else up, device_id_type=MESH)

    every = pl.ds(0, chans)

    def wait_sent(j, slot):
        @pl.when(has_up)
        def _():
            y_copy(j, slot, 0, every).wait_send()

        @pl.when(has_down)
        def _():
            y_copy(j, slot, 1, every).wait_send()

    def x_pass(j, slot, waits):
        own = CHUNK * TILE

        @pl.loop(0, GROUPS)
        def _(g):
            for cond, copy in waits:
                if cond is None:
                    copy(g).wait()
                else:
                    @pl.when(cond)
                    def _():
                        copy(g).wait_recv()

            @pl.loop(0, per_group // 2)
            def _(p):
                c = g * per_group + 2 * p
                for t in range(2):
                    pair = [vext[c + i, pl.ds(j * CHUNK, window), pl.ds(t * TILE, TILE)].reshape(window * TILE, depth)
                            for i in range(2)]
                    got = jnp.dot(ax[t], jnp.concatenate(pair, axis=1), preferred_element_type=jnp.float32)
                    got = got.astype(jnp.bfloat16)
                    for i in range(2):
                        part = got[:, i * depth:(i + 1) * depth]
                        u1[c + i, pl.ds(j * CHUNK, CHUNK), pl.ds(t * TILE, TILE)] = part[:own].reshape(CHUNK, TILE, depth)
                        send[slot, t, c + i] = part[own:]

            cs = pl.ds(g * per_group, per_group)

            @pl.when(has_up)
            def _():
                y_copy(j, slot, 0, cs).start()

            @pl.when(has_down)
            def _():
                y_copy(j, slot, 1, cs).start()

    def out_copy(s, x):
        return pltpu.make_async_copy(stage.at[s], out_hbm.at[:, x], out_sem.at[s])

    def yz_mix(j, first):
        slot = 0

        @pl.when(has_up)
        def _():
            y_copy(j, slot, 1, every).wait_recv()

        @pl.when(has_down)
        def _():
            y_copy(j, slot, 0, every).wait_recv()

        chunk = pl.ds(j * CHUNK, CHUNK)

        @pl.loop(0, chans // 4)
        def _(q):
            for h in range(2):
                c = 4 * q + 2 * h
                own = jnp.concatenate([u1[c + i, chunk].reshape(CHUNK * extent, depth) for i in range(2)], axis=1)
                top = jnp.concatenate([recv[j, 0, c + i] for i in range(2)], axis=1)
                bot = jnp.concatenate([recv[j, 1, c + i] for i in range(2)], axis=1)
                rhs = jnp.concatenate([own, top, bot], axis=0)
                u2 = jnp.dot(ay[...], rhs, preferred_element_type=jnp.float32).astype(jnp.bfloat16)
                u3 = jnp.dot(u2, bz[...], preferred_element_type=jnp.float32).astype(jnp.bfloat16)
                for i in range(2):
                    u1[c + i, chunk] = u3[:, i * depth:(i + 1) * depth].reshape(CHUNK, extent, depth)

        @pl.loop(0, CHUNK // 2)
        def _(i):
            for s in range(2):
                x = j * CHUNK + 2 * i + s
                if first:
                    @pl.when(i > 0)
                    def _():
                        out_copy(s, x).wait()
                else:
                    out_copy(s, x).wait()
                rhs = jnp.concatenate(
                    [u1[:, x, pl.ds(t * TILE, TILE)].reshape(chans * TILE, depth) for t in range(2)], axis=1)
                step = 256
                for m in range(chans * TILE // step):
                    acc = jnp.dot(wk[pl.ds(m * step, step)], rhs, preferred_element_type=jnp.float32)
                    cs = pl.ds(m * (step // TILE), step // TILE)
                    for t in range(2):
                        pre = acc[:, t * depth:(t + 1) * depth] + bias[pl.ds(m * step, step)]
                        old = vext[cs, half + x, pl.ds(t * TILE, TILE)].reshape(step, depth).astype(jnp.float32)
                        new = (old + gelu(pre)).astype(jnp.bfloat16)
                        stage[s, cs, pl.ds(t * TILE, TILE)] = new.reshape(step // TILE, TILE, depth)
                out_copy(s, x).start()

    from_left = (has_left, lambda g: x_copy(True, False, g))
    from_right = (has_right, lambda g: x_copy(False, False, g))
    far_left = (has_left, lambda g: x_copy(True, True, g))
    far_right = (has_right, lambda g: x_copy(False, True, g))

    x_pass(1, 0, [(None, load), from_left])
    x_pass(2, 1, [from_right])
    yz_mix(1, True)
    wait_sent(1, 0)
    x_pass(0, 0, [far_left])
    wait_sent(2, 1)
    x_pass(3, 1, [far_right])

    @pl.loop(0, 3)
    def _(k):
        yz_mix(lax.rem(2 + 3 * k, 5), False)

    wait_sent(0, 0)
    wait_sent(3, 1)
    for is_far in (False, True):
        for g in range(GROUPS):
            @pl.when(has_right)
            def _():
                x_copy(True, is_far, g).wait_send()

            @pl.when(has_left)
            def _():
                x_copy(False, is_far, g).wait_send()
    for s in range(2):
        out_copy(s, s).wait()


def solution(mesh):
    nx, ny = mesh.shape[ROW_AXIS], mesh.shape[COL_AXIS]
    vol_spec = P(PARTS_AXIS, ROW_AXIS, COL_AXIS, None)

    def local_layers(volume, filter_taps, mix_weights, mix_bias):
        chans, planes, extent, depth = volume.shape
        half = (filter_taps.shape[2] - 1) // 2
        slab = CHUNK * half
        mats = matrices(filter_taps, mix_weights, mix_bias, extent, depth)
        bf = jnp.bfloat16
        current = volume
        for layer in range(filter_taps.shape[0]):
            current = pl.pallas_call(
                functools.partial(layer_kernel, layer, nx, ny, half),
                out_shape=jax.ShapeDtypeStruct(volume.shape, bf),
                in_specs=[pl.BlockSpec(memory_space=pl.ANY)] * 7,
                out_specs=pl.BlockSpec(memory_space=pl.ANY),
                scratch_shapes=[
                    pltpu.VMEM((chans, planes + 2 * half, extent, depth), bf),
                    pltpu.VMEM(volume.shape, bf),
                    pltpu.VMEM((2, 2, chans, slab, depth), bf),
                    pltpu.VMEM((planes // CHUNK, 2, chans, slab, depth), bf),
                    pltpu.VMEM((2, chans, extent, depth), bf),
                    pltpu.VMEM((2,) + mats[0].shape[1:], bf),
                    pltpu.VMEM(mats[2].shape[1:], bf),
                    pltpu.VMEM(mats[3].shape[1:], bf),
                    pltpu.VMEM(mats[4].shape[1:], bf),
                    pltpu.VMEM(mats[5].shape[1:], jnp.float32),
                    pltpu.SemaphoreType.DMA((GROUPS,)),
                    pltpu.SemaphoreType.DMA((6,)),
                    pltpu.SemaphoreType.DMA((2, 2, GROUPS)),
                    pltpu.SemaphoreType.DMA((2, 2, GROUPS)),
                    pltpu.SemaphoreType.DMA((2, 2)),
                    pltpu.SemaphoreType.DMA((planes // CHUNK, 2)),
                    pltpu.SemaphoreType.DMA((2,)),
                ],
                compiler_params=pltpu.CompilerParams(
                    collective_id=layer, has_side_effects=True, vmem_limit_bytes=67043328),
                name=f"layer_{layer}",
            )(current, *mats)
        return current

    return jax.shard_map(local_layers, mesh=mesh, in_specs=(vol_spec, P(), P(), P()), out_specs=vol_spec, check_vma=False)
```

time: 1150 us -> 455 us (0.40)
  waiting for transfers between devices: 437 us -> 0 us
  Pallas kernels: 0 us -> 434 us
  matrix products: 401 us -> 0 us
  local copies, waits for them, and re-layouts: 182 us -> 15.8 us
  other arithmetic: 94.3 us -> 1.28 us
  starting transfers between devices: 29.4 us -> 0 us
    ppermute x12 -> x0, waiting for transfers between devices: 437 us -> none  [the longest x6 409 us: halo_pass(): lax.ppermute(head_planes, axis_name, [(source + 1, source) for source in...]
    pallas_call x0 -> x4, Pallas kernels: none -> 434 us  [the longest x3 422 us: local_layers(): pl.pallas_call(functools.partial(layer_kernel, layer, nx, ny, half), out_...]
    dot_general x9 -> x0, matrix products: 401 us -> none  [the longest x6 248 us: halo_pass(): jnp.einsum(eq_form, padded, toeplitz, preferred_element_type=jnp.float32)]
    concatenate x5 -> x0, other arithmetic: 94.2 us -> none  [halo_pass(): padded = jnp.concatenate([from_left, operand, from_right], axis=dim_index)]
    slice x6 -> x0, local copies, waits for them, and re-layouts: 63.8 us -> none  [halo_pass(): lax.slice_in_dim(operand, extent - half_width, extent, axis=dim_index)]
    gather x16 -> x0, local copies, waits for them, and re-layouts: 62.1 us -> none  [band_matrix(): tap_row.astype(jnp.bfloat16)[jnp.clip(tap_index, 0, tap_count - 1)]]
    ppermute x12 -> x0, starting transfers between devices: 29.4 us -> none  [the longest x6 17.8 us: halo_pass(): lax.ppermute(head_planes, axis_name, [(source + 1, source) for source in...]
    ppermute x2 -> x0, local copies, waits for them, and re-layouts: 22.1 us -> none  [the longest x1 11.1 us: halo_pass(): lax.ppermute(head_planes, axis_name, [(source + 1, source) for source in...]
  transfers between devices with their start and end apart: 12 -> 0, of which waited for: 11 -> 0; matrix products, arithmetic and copies ran while one was open for 8% -> 0% of each run, Pallas kernels for 0% -> 0%
where the time goes in v1:
time: 455 us; the launch traced here: 451 us
  Pallas kernels  434 us (95%)
  local copies, waits for them, and re-layouts  15.8 us (3%)
    pallas_call x3, Pallas kernels, local_layers(): pl.pallas_call(functools.partial(layer_kernel, layer, nx, ny, half), out_...  422 us
    unnamed x1, local copies, waits for them, and re-layouts  14.5 us
    pallas_call x1, Pallas kernels, matrices(): pl.pallas_call(matrices_kernel, grid=(layers,), out_shape=outs, in_specs=...  11.4 us

profile of v1, /device:TPU:122, one launch (start us, length us, event | category | flops | bytes accessed | tf_op | source)
XLA Modules:
  0.0 450.8 jit_solution(17719471574269828756)
XLA Ops:
  0.0 1.2 broadcast_in_dim.3.bias_col
  1.2 1.3 reduce_precision.3.taps
  2.5 11.4 %matrices.1 = (bf16[3,208,448]{2,1,0:T(8,128)(2,1)}, bf16[3,208,448]{2,1,0:T(8,128)(2,1)}, bf16[3,256,416]{2,1,0:T(8,128)(2,1)}, bf16[3,256,256]{2,1,0:T(8,128)(...) custom-call(f32[3,3,21]{2,1,0:T(4,128)} %reduce_precision.3.taps, bf16[3,64,64]{2,1,0:T(8,128)(2,1)} %weights.1, ...), custom_call_target="tpu_custom_call" | custom-call | tf_op jit(solution)/shard_map/matrices/pallas_call | solution.py:96
  13.9 141.0 %layer_0.1.v_hbm = bf16[64,32,32,128]{3,2,1,0:T(8,128)(2,1)} custom-call(bf16[64,32,32,128]{3,2,1,0:T(8,128)(2,1)} %v_hbm.1, bf16[3,208,448]{2,1,0:T(8,128)(2,1)} %get-tuple-element.11.ax0_hbm, bf16[3,208,448]{2,1,0:T(8,128)(2,1)} %get-tuple-element.12.ax1_hbm, bf16[3,256,416]{2,1,0:T(8,128)(2,1)} %get-tuple-element.13.ay_hbm, ...), custom_call_target="tpu_custom_call" | custom-call | tf_op jit(solution)/shard_map/layer_0/pallas_call | solution.py:345
  154.9 141.8 %layer_1.1.v_hbm = bf16[64,32,32,128]{3,2,1,0:T(8,128)(2,1)} custom-call(bf16[64,32,32,128]{3,2,1,0:T(8,128)(2,1)} %layer_0.1.v_hbm, bf16[3,208,448]{2,1,0:T(8,128)(2,1)} %get-tuple-element.11.ax0_hbm, bf16[3,208,448]{2,1,0:T(8,128)(2,1)} %get-tuple-element.12.ax1_hbm, bf16[3,256,416]{2,1,0:T(8,128)(2,1)} %get-tuple-element.13.ay_hbm, ...), custom_call_target="tpu_custom_call" | custom-call | tf_op jit(solution)/shard_map/layer_1/pallas_call | solution.py:345
  296.7 139.5 %layer_2.1 = bf16[64,32,32,128]{3,2,1,0:T(8,128)(2,1)} custom-call(bf16[64,32,32,128]{3,2,1,0:T(8,128)(2,1)} %layer_1.1.v_hbm, bf16[3,208,448]{2,1,0:T(8,128)(2,1)} %get-tuple-element.11.ax0_hbm, bf16[3,208,448]{2,1,0:T(8,128)(2,1)} %get-tuple-element.12.ax1_hbm, bf16[3,256,416]{2,1,0:T(8,128)(2,1)} %get-tuple-element.13.ay_hbm, ...), custom_call_target="tpu_custom_call" | custom-call | tf_op jit(solution)/shard_map/layer_2/pallas_call | solution.py:345
  436.2 14.5 %copy.6 = bf16[64,32,32,128]{3,2,1,0:T(8,128)(2,1)} copy(bf16[64,32,32,128]{3,2,1,0:T(8,128)(2,1)} %layer_2.1) | data formatting | bytes 33554432

commit v2 on v0

v2 whole, which is shorter than its diff:
```python
import functools

import jax
import jax.numpy as jnp
from jax import lax
from jax.experimental import pallas as pl
from jax.experimental.pallas import tpu as pltpu
from jax.sharding import PartitionSpec as P

PARTS_AXIS = "batch"
COL_AXIS = "ysp"
ROW_AXIS = "xsp"
MESH = pl.DeviceIdType.MESH
TILE = 16
CHUNK = 4
GROUPS = 4
SLOTS = 5


def rows_cols(n_rows, n_cols):
    shape = (n_rows, n_cols)
    return lax.broadcasted_iota(jnp.int32, shape, 0), lax.broadcasted_iota(jnp.int32, shape, 1)


def banded(tap, n_taps, tap_index, valid):
    index = jnp.where(valid, tap_index, -1)
    total = jnp.zeros(index.shape, jnp.float32)
    for t in range(n_taps):
        total = jnp.where(index == t, tap(t), total)
    return total.astype(jnp.bfloat16)


def x_matrix(tap, n_taps, last_tile):
    half = (n_taps - 1) // 2
    own = CHUNK * TILE
    r, k = rows_cols(own + CHUNK * half, (CHUNK + 2 * half) * TILE)
    s = jnp.maximum(r - own, 0)
    plane = jnp.where(r < own, r // TILE, s // half)
    row = jnp.where(r < own, r % TILE, s % half + (TILE - half if last_tile else 0))
    return banded(tap, n_taps, k // TILE - plane, row == k % TILE)


def y_matrix(tap, n_taps, extent):
    half = (n_taps - 1) // 2
    own, slab = CHUNK * extent, CHUNK * half
    r, k = rows_cols(own, own + 2 * slab)
    s = jnp.maximum(jnp.where(k < own + slab, k - own, k - own - slab), 0)
    plane = jnp.where(k < own, k // extent, s // half)
    pos = jnp.where(k < own, k % extent + half, jnp.where(k < own + slab, s % half, s % half + half + extent))
    return banded(tap, n_taps, pos - r % extent, plane == r // extent)


def z_matrix(tap, n_taps, depth):
    r, k = rows_cols(2 * depth, 2 * depth)
    return banded(tap, n_taps, r % depth - k % depth + (n_taps - 1) // 2, r // depth == k // depth)


def gelu(v):
    c0 = 0.7978845608028654
    arg = v * (c0 + (c0 * 0.044715) * (v * v))
    h = 0.5 * v
    return h + h * jnp.tanh(arg)


def stack_kernel(nx, ny, v_hbm, taps, weights, biases, out_hbm, vext, u1, send, recv, ax, ay, bz, wk, bias,
                 load_sem, xsend, xrecv, ysend, yrecv, out_sem, ycred, xcred):
    chans, planes, extent, depth = u1.shape
    n_layers, _, n_taps = taps.shape
    half = (n_taps - 1) // 2
    n_chunks = planes // CHUNK
    middle = n_chunks // 2
    per_group = chans // GROUPS
    slab = CHUNK * half
    window = CHUNK + 2 * half
    near = half - 2 * CHUNK
    bi, yi, xi = lax.axis_index(PARTS_AXIS), lax.axis_index(COL_AXIS), lax.axis_index(ROW_AXIS)
    left = (bi, yi, lax.rem(xi + nx - 1, nx))
    right = (bi, yi, lax.rem(xi + 1, nx))
    up = (bi, lax.rem(yi + ny - 1, ny), xi)
    down = (bi, lax.rem(yi + 1, ny), xi)
    has_left, has_right, has_up, has_down = xi > 0, xi < nx - 1, yi > 0, yi < ny - 1
    beside = ((has_left, left), (has_right, right))
    above = ((has_up, up), (has_down, down))

    def chunk_of(n):
        low = middle - 1 - n // 2
        return low + (n % 2) * (1 + 2 * (n // 2))

    def load(g):
        cs = pl.ds(g * per_group, per_group)
        return pltpu.make_async_copy(v_hbm.at[cs], vext.at[cs, pl.ds(half, planes)], load_sem.at[g])

    pieces = ((0, near), (near, CHUNK - near), (CHUNK, CHUNK), (2 * CHUNK, near))

    def x_copy(side, piece, layer):
        first, n = pieces[piece]
        src = planes - first - n if side else first
        dst = src + half - planes if side else src + half + planes
        source = v_hbm.at[:, pl.ds(src, n)] if layer == 0 else vext.at[:, pl.ds(half + src, n)]
        return pltpu.make_async_remote_copy(
            src_ref=source, dst_ref=vext.at[:, pl.ds(dst, n)],
            send_sem=xsend.at[side, piece], recv_sem=xrecv.at[side, piece],
            device_id=beside[side][1], device_id_type=MESH)

    def x_start(side, which, layer):
        @pl.when(beside[side][0])
        def _():
            for piece in which:
                x_copy(side, piece, layer).start()

    def y_copy(k, slot, side, g):
        cs = pl.ds(g * per_group, per_group)
        return pltpu.make_async_remote_copy(
            src_ref=send.at[slot, side, cs], dst_ref=recv.at[k, cs, pl.ds((1 - side) * slab, slab)],
            send_sem=ysend.at[slot, side, g], recv_sem=yrecv.at[k, 1 - side, g],
            device_id=above[side][1], device_id_type=MESH)

    def set_x_matrices(layer):
        for t in range(2):
            ax[t] = x_matrix(lambda i: taps[layer, 0, i], n_taps, t == 1)

    def set_other_matrices(layer):
        ay[...] = y_matrix(lambda i: taps[layer, 1, i], n_taps, extent)
        bz[...] = z_matrix(lambda i: taps[layer, 2, i], n_taps, depth)
        block = 128

        @pl.loop(0, chans * TILE // block)
        def _(b):
            r, k = rows_cols(chans, chans * TILE)
            across = (k // TILE == r).astype(jnp.bfloat16)
            wide = jnp.dot(weights[layer].T, across, preferred_element_type=jnp.float32).astype(jnp.bfloat16)
            m, c = rows_cols(block, chans)
            mine = (m + b * block) // TILE == c
            full = jnp.dot(mine.astype(jnp.bfloat16), wide, preferred_element_type=jnp.float32)
            m, k = rows_cols(block, chans * TILE)
            at = pl.ds(pl.multiple_of(b * block, block), block)
            wk[at] = jnp.where(m % TILE == k % TILE, full, 0.0).astype(jnp.bfloat16)
            spread = jnp.sum(jnp.where(mine, biases[pl.ds(layer, 1)], 0.0), axis=1, keepdims=True)
            bias[at] = jnp.broadcast_to(spread, (block, depth))

    def x_pass(layer, n):
        k = chunk_of(n)
        own = CHUNK * TILE
        turn = n_chunks * layer + n
        slot = turn % SLOTS
        side = n % 2
        reach = {1: (0,), 2: (1, 2), 3: (3,)}.get(n // 2, ())
        if reach:
            @pl.when(beside[side][0])
            def _():
                for piece in reach:
                    x_copy(1 - side, piece, layer).wait_recv()
        for s in range(2):
            @pl.when(above[s][0])
            def _():
                if turn >= SLOTS:
                    for g in range(GROUPS):
                        y_copy(chunk_of((turn - SLOTS) % n_chunks), slot, s, g).wait_send()
                if layer > 0:
                    pl.semaphore_wait(ycred.at[s], 1)

        @pl.loop(0, GROUPS)
        def _(g):
            if turn == 0:
                load(g).wait()

            @pl.loop(0, per_group // 2)
            def _(p):
                c = g * per_group + 2 * p
                for t in range(2):
                    pair = [vext[c + i, pl.ds(k * CHUNK, window), pl.ds(t * TILE, TILE)].reshape(window * TILE, depth)
                            for i in range(2)]
                    got = jnp.dot(ax[t], jnp.concatenate(pair, axis=1), preferred_element_type=jnp.float32)
                    got = got.astype(jnp.bfloat16)
                    for i in range(2):
                        part = got[:, i * depth:(i + 1) * depth]
                        u1[c + i, pl.ds(k * CHUNK, CHUNK), pl.ds(t * TILE, TILE)] = part[:own].reshape(CHUNK, TILE, depth)
                        send[slot, t, c + i] = part[own:]

            for s in range(2):
                @pl.when(above[s][0])
                def _():
                    y_copy(k, slot, s, g).start()

        if n >= n_chunks - 2 and layer < n_layers - 1:
            @pl.when(beside[side][0])
            def _():
                pl.semaphore_signal(xcred.at[1 - side], inc=1, device_id=beside[side][1], device_id_type=MESH)

    def out_copy(k):
        return pltpu.make_async_copy(
            vext.at[:, pl.ds(half + k * CHUNK, CHUNK)], out_hbm.at[:, pl.ds(k * CHUNK, CHUNK)], out_sem.at[k])

    def yz_mix(layer, n):
        k = chunk_of(n)
        chunk = pl.ds(k * CHUNK, CHUNK)

        @pl.loop(0, GROUPS)
        def _(g):
            for s in range(2):
                @pl.when(above[1 - s][0])
                def _():
                    y_copy(k, 0, s, g).wait_recv()

            @pl.loop(0, per_group // 8)
            def _(q):
                for h in range(4):
                    c = g * per_group + 8 * q + 2 * h
                    own = jnp.concatenate([u1[c + i, chunk].reshape(CHUNK * extent, depth) for i in range(2)], axis=1)
                    halo = jnp.concatenate([recv[k, c + i] for i in range(2)], axis=1)
                    rhs = jnp.concatenate([own, halo], axis=0)
                    u2 = jnp.dot(ay[...], rhs, preferred_element_type=jnp.float32).astype(jnp.bfloat16)
                    u3 = jnp.dot(u2, bz[...], preferred_element_type=jnp.float32).astype(jnp.bfloat16)
                    for i in range(2):
                        u1[c + i, chunk] = u3[:, i * depth:(i + 1) * depth].reshape(CHUNK, extent, depth)

        if layer < n_layers - 1:
            for s in range(2):
                @pl.when(above[s][0])
                def _():
                    pl.semaphore_signal(ycred.at[1 - s], inc=1, device_id=above[s][1], device_id_type=MESH)

        @pl.loop(0, CHUNK // 2)
        def _(i):
            for s in range(2):
                x = k * CHUNK + 2 * i + s
                rhs = jnp.concatenate(
                    [u1[:, x, pl.ds(t * TILE, TILE)].reshape(chans * TILE, depth) for t in range(2)], axis=1)
                step = 256
                for m in range(chans * TILE // step):
                    acc = jnp.dot(wk[pl.ds(m * step, step)], rhs, preferred_element_type=jnp.float32)
                    cs = pl.ds(m * (step // TILE), step // TILE)
                    for t in range(2):
                        at = (cs, half + x, pl.ds(t * TILE, TILE))
                        pre = acc[:, t * depth:(t + 1) * depth] + bias[pl.ds(m * step, step)]
                        old = vext[at].reshape(step, depth).astype(jnp.float32)
                        vext[at] = (old + gelu(pre)).astype(jnp.bfloat16).reshape(step // TILE, TILE, depth)

        if layer == n_layers - 1:
            out_copy(k).start()

    def send_halo(layer, n):
        side, which = n % 2, {1: (3,), 2: (2,), 3: (0, 1)}[n // 2]
        if n // 2 == 1:
            @pl.when(beside[side][0])
            def _():
                pl.semaphore_wait(xcred.at[side], 1)
        x_start(side, which, layer + 1)

    for g in range(GROUPS):
        load(g).start()
    barrier = pltpu.get_barrier_semaphore()
    for dev in (left, right, up, down):
        pl.semaphore_signal(barrier, inc=1, device_id=dev, device_id_type=MESH)
    pl.semaphore_wait(barrier, 4)
    for piece in range(4):
        for side in range(2):
            x_start(side, (piece,), 0)
    set_x_matrices(0)
    x_pass(0, 0)

    for side in range(2):
        @pl.when(jnp.logical_not(beside[side][0]))
        def _():
            @pl.loop(0, chans)
            def _(c):
                vext[c, pl.ds(side * (half + planes), half)] = jnp.zeros((half, extent, depth), jnp.bfloat16)

        @pl.when(jnp.logical_not(above[side][0]))
        def _():
            @pl.loop(0, chans)
            def _(c):
                for k in range(n_chunks):
                    recv[k, c, pl.ds(side * slab, slab)] = jnp.zeros((slab, depth), jnp.bfloat16)

    last = n_chunks - 1
    for layer in range(n_layers):
        for n in range(1, n_chunks):
            x_pass(layer, n)
        for side in range(2):
            @pl.when(beside[side][0])
            def _():
                for piece in range(4):
                    x_copy(side, piece, layer).wait_send()
        if layer < n_layers - 1:
            set_x_matrices(layer + 1)
        set_other_matrices(layer)

        @pl.loop(0, last)
        def _(n):
            yz_mix(layer, n)
            if layer < n_layers - 1:
                for m in range(2, last):
                    @pl.when(n == m)
                    def _():
                        send_halo(layer, m)

        if layer < n_layers - 1:
            x_pass(layer + 1, 0)
        yz_mix(layer, last)
        if layer < n_layers - 1:
            send_halo(layer, last)

    turns = n_chunks * n_layers
    for turn in range(max(0, turns - SLOTS), turns):
        for s in range(2):
            @pl.when(above[s][0])
            def _():
                for g in range(GROUPS):
                    y_copy(chunk_of(turn % n_chunks), turn % SLOTS, s, g).wait_send()
    for k in range(n_chunks):
        out_copy(k).wait()


def solution(mesh):
    nx, ny = mesh.shape[ROW_AXIS], mesh.shape[COL_AXIS]
    vol_spec = P(PARTS_AXIS, ROW_AXIS, COL_AXIS, None)

    def local_layers(volume, filter_taps, mix_weights, mix_bias):
        chans, planes, extent, depth = volume.shape
        half = (filter_taps.shape[2] - 1) // 2
        n_chunks, slab = planes // CHUNK, CHUNK * half
        bf = jnp.bfloat16
        return pl.pallas_call(
            functools.partial(stack_kernel, nx, ny),
            out_shape=jax.ShapeDtypeStruct(volume.shape, bf),
            in_specs=[pl.BlockSpec(memory_space=pl.ANY), pl.BlockSpec(memory_space=pltpu.SMEM),
                      pl.BlockSpec(memory_space=pltpu.VMEM), pl.BlockSpec(memory_space=pltpu.VMEM)],
            out_specs=pl.BlockSpec(memory_space=pl.ANY),
            scratch_shapes=[
                pltpu.VMEM((chans, planes + 2 * half, extent, depth), bf),
                pltpu.VMEM(volume.shape, bf),
                pltpu.VMEM((SLOTS, 2, chans, slab, depth), bf),
                pltpu.VMEM((n_chunks, chans, 2 * slab, depth), bf),
                pltpu.VMEM((2, CHUNK * TILE + slab, (CHUNK + 2 * half) * TILE), bf),
                pltpu.VMEM((CHUNK * extent, CHUNK * extent + 2 * slab), bf),
                pltpu.VMEM((2 * depth, 2 * depth), bf),
                pltpu.VMEM((chans * TILE, chans * TILE), bf),
                pltpu.VMEM((chans * TILE, depth), jnp.float32),
                pltpu.SemaphoreType.DMA((GROUPS,)),
                pltpu.SemaphoreType.DMA((2, 4)),
                pltpu.SemaphoreType.DMA((2, 4)),
                pltpu.SemaphoreType.DMA((SLOTS, 2, GROUPS)),
                pltpu.SemaphoreType.DMA((n_chunks, 2, GROUPS)),
                pltpu.SemaphoreType.DMA((n_chunks,)),
                pltpu.SemaphoreType.REGULAR((2,)),
                pltpu.SemaphoreType.REGULAR((2,)),
            ],
            compiler_params=pltpu.CompilerParams(
                collective_id=0, has_side_effects=True, vmem_limit_bytes=67043328),
            name="stack",
        )(volume, filter_taps, mix_weights, mix_bias)

    return jax.shard_map(local_layers, mesh=mesh, in_specs=(vol_spec, P(), P(), P()), out_specs=vol_spec, check_vma=False)
```

time: 1150 us -> 392 us (0.34)
  waiting for transfers between devices: 437 us -> 0 us
  matrix products: 401 us -> 0 us
  Pallas kernels: 0 us -> 373 us
  local copies, waits for them, and re-layouts: 182 us -> 14.5 us
  other arithmetic: 94.3 us -> 0 us
  starting transfers between devices: 29.4 us -> 0 us
    ppermute x12 -> x0, waiting for transfers between devices: 437 us -> none  [the longest x6 409 us: halo_pass(): lax.ppermute(head_planes, axis_name, [(source + 1, source) for source in...]
    dot_general x9 -> x0, matrix products: 401 us -> none  [the longest x6 248 us: halo_pass(): jnp.einsum(eq_form, padded, toeplitz, preferred_element_type=jnp.float32)]
    pallas_call x0 -> x1, Pallas kernels: none -> 373 us  [local_layers(): pl.pallas_call(functools.partial(stack_kernel, nx, ny), out_shape=jax.Sha...]
    concatenate x5 -> x0, other arithmetic: 94.2 us -> none  [halo_pass(): padded = jnp.concatenate([from_left, operand, from_right], axis=dim_index)]
    slice x6 -> x0, local copies, waits for them, and re-layouts: 63.8 us -> none  [halo_pass(): lax.slice_in_dim(operand, extent - half_width, extent, axis=dim_index)]
    gather x16 -> x0, local copies, waits for them, and re-layouts: 62.1 us -> none  [band_matrix(): tap_row.astype(jnp.bfloat16)[jnp.clip(tap_index, 0, tap_count - 1)]]
    ppermute x12 -> x0, starting transfers between devices: 29.4 us -> none  [the longest x6 17.8 us: halo_pass(): lax.ppermute(head_planes, axis_name, [(source + 1, source) for source in...]
    ppermute x2 -> x0, local copies, waits for them, and re-layouts: 22.1 us -> none  [the longest x1 11.1 us: halo_pass(): lax.ppermute(head_planes, axis_name, [(source + 1, source) for source in...]
  transfers between devices with their start and end apart: 12 -> 0, of which waited for: 11 -> 0; matrix products, arithmetic and copies ran while one was open for 8% -> 0% of each run, Pallas kernels for 0% -> 0%
where the time goes in v2:
time: 392 us; the launch traced here: 388 us
  Pallas kernels  373 us (95%)
  local copies, waits for them, and re-layouts  14.5 us (4%)
    pallas_call x1, Pallas kernels, local_layers(): pl.pallas_call(functools.partial(stack_kernel, nx, ny), out_shape=jax.Sha...  373 us
    unnamed x1, local copies, waits for them, and re-layouts  14.5 us

profile of v2, /device:TPU:122, one launch (start us, length us, event | category | flops | bytes accessed | tf_op | source)
XLA Modules:
  0.0 388.0 jit_solution(536538376192778362)
XLA Ops:
  0.0 373.5 %stack.1 = bf16[64,32,32,128]{3,2,1,0:T(8,128)(2,1)} custom-call(bf16[64,32,32,128]{3,2,1,0:T(8,128)(2,1)} %v_hbm.1, f32[3,3,21]{2,1,0:T(4,128)} %taps.1, bf16[3,64,64]{2,1,0:T(8,128)(2,1)} %weights.1, f32[3,64]{1,0:T(4,128)} %biases.1), custom_call_target="tpu_custom_call" | custom-call | tf_op jit(solution)/shard_map/stack/pallas_call | solution.py:324
  373.5 14.5 %copy.6 = bf16[64,32,32,128]{3,2,1,0:T(8,128)(2,1)} copy(bf16[64,32,32,128]{3,2,1,0:T(8,128)(2,1)} %stack.1) | data formatting | bytes 33554432

commit v3 on v2

--- a/solution.py
+++ b/solution.py
@@ -62,8 +62,8 @@
     return h + h * jnp.tanh(arg)
 
 
-def stack_kernel(nx, ny, v_hbm, taps, weights, biases, out_hbm, vext, u1, send, recv, ax, ay, bz, wk, bias,
-                 load_sem, xsend, xrecv, ysend, yrecv, out_sem, ycred, xcred):
+def stack_kernel(nx, ny, v_hbm, taps, weights, biases, u1, vext, send, recv, ax, ay, bz, wk, bias,
+                 load_sem, xsend, xrecv, ysend, yrecv, ycred, xcred):
     chans, planes, extent, depth = u1.shape
     n_layers, _, n_taps = taps.shape
     half = (n_taps - 1) // 2
@@ -82,9 +82,13 @@
     beside = ((has_left, left), (has_right, right))
     above = ((has_up, up), (has_down, down))
 
+    def side_of(n):
+        m, b = n // 2, n % 2
+        swap = m * (middle - 1 - m) // 2
+        return b + swap - 2 * b * swap
+
     def chunk_of(n):
-        low = middle - 1 - n // 2
-        return low + (n % 2) * (1 + 2 * (n // 2))
+        return middle - 1 - n // 2 + side_of(n) * (1 + 2 * (n // 2))
 
     def load(g):
         cs = pl.ds(g * per_group, per_group)
@@ -143,7 +147,7 @@
         own = CHUNK * TILE
         turn = n_chunks * layer + n
         slot = turn % SLOTS
-        side = n % 2
+        side = side_of(n)
         reach = {1: (0,), 2: (1, 2), 3: (3,)}.get(n // 2, ())
         if reach:
             @pl.when(beside[side][0])
@@ -187,11 +191,7 @@
             def _():
                 pl.semaphore_signal(xcred.at[1 - side], inc=1, device_id=beside[side][1], device_id_type=MESH)
 
-    def out_copy(k):
-        return pltpu.make_async_copy(
-            vext.at[:, pl.ds(half + k * CHUNK, CHUNK)], out_hbm.at[:, pl.ds(k * CHUNK, CHUNK)], out_sem.at[k])
-
-    def yz_mix(layer, n):
+    def yz_pass(layer, n):
         k = chunk_of(n)
         chunk = pl.ds(k * CHUNK, CHUNK)
 
@@ -219,6 +219,9 @@
                 @pl.when(above[s][0])
                 def _():
                     pl.semaphore_signal(ycred.at[1 - s], inc=1, device_id=above[s][1], device_id_type=MESH)
+
+    def mix(layer, n):
+        k = chunk_of(n)
 
         @pl.loop(0, CHUNK // 2)
         def _(i):
@@ -237,10 +240,12 @@
                         vext[at] = (old + gelu(pre)).astype(jnp.bfloat16).reshape(step // TILE, TILE, depth)
 
         if layer == n_layers - 1:
-            out_copy(k).start()
+            @pl.loop(0, chans)
+            def _(c):
+                u1[c, pl.ds(k * CHUNK, CHUNK)] = vext[c, pl.ds(half + k * CHUNK, CHUNK)]
 
     def send_halo(layer, n):
-        side, which = n % 2, {1: (3,), 2: (2,), 3: (0, 1)}[n // 2]
+        side, which = side_of(n), {1: (3,), 2: (2,), 3: (0, 1)}[n // 2]
         if n // 2 == 1:
             @pl.when(beside[side][0])
             def _():
@@ -274,8 +279,17 @@
                     recv[k, c, pl.ds(side * slab, slab)] = jnp.zeros((slab, depth), jnp.bfloat16)
 
     last = n_chunks - 1
+    early = 2
     for layer in range(n_layers):
-        for n in range(1, n_chunks):
+        for n in range(1, n_chunks - 2):
+            x_pass(layer, n)
+        set_other_matrices(layer)
+
+        @pl.loop(0, early)
+        def _(n):
+            yz_pass(layer, n)
+
+        for n in range(n_chunks - 2, n_chunks):
             x_pass(layer, n)
         for side in range(2):
             @pl.when(beside[side][0])
@@ -284,11 +298,14 @@
                     x_copy(side, piece, layer).wait_send()
         if layer < n_layers - 1:
             set_x_matrices(layer + 1)
-        set_other_matrices(layer)
 
         @pl.loop(0, last)
         def _(n):
-            yz_mix(layer, n)
+            @pl.when(n >= early)
+            def _():
+                yz_pass(layer, n)
+
+            mix(layer, n)
             if layer < n_layers - 1:
                 for m in range(2, last):
                     @pl.when(n == m)
@@ -297,7 +314,8 @@
 
         if layer < n_layers - 1:
             x_pass(layer + 1, 0)
-        yz_mix(layer, last)
+        yz_pass(layer, last)
+        mix(layer, last)
         if layer < n_layers - 1:
             send_halo(layer, last)
 
@@ -308,8 +326,6 @@
             def _():
                 for g in range(GROUPS):
                     y_copy(chunk_of(turn % n_chunks), turn % SLOTS, s, g).wait_send()
-    for k in range(n_chunks):
-        out_copy(k).wait()
 
 
 def solution(mesh):
@@ -323,13 +339,12 @@
         bf = jnp.bfloat16
         return pl.pallas_call(
             functools.partial(stack_kernel, nx, ny),
-            out_shape=jax.ShapeDtypeStruct(volume.shape, bf),
+            out_shape=pltpu.VMEM(volume.shape, bf),
             in_specs=[pl.BlockSpec(memory_space=pl.ANY), pl.BlockSpec(memory_space=pltpu.SMEM),
                       pl.BlockSpec(memory_space=pltpu.VMEM), pl.BlockSpec(memory_space=pltpu.VMEM)],
-            out_specs=pl.BlockSpec(memory_space=pl.ANY),
+            out_specs=pl.BlockSpec(memory_space=pltpu.VMEM),
             scratch_shapes=[
                 pltpu.VMEM((chans, planes + 2 * half, extent, depth), bf),
-                pltpu.VMEM(volume.shape, bf),
                 pltpu.VMEM((SLOTS, 2, chans, slab, depth), bf),
                 pltpu.VMEM((n_chunks, chans, 2 * slab, depth), bf),
                 pltpu.VMEM((2, CHUNK * TILE + slab, (CHUNK + 2 * half) * TILE), bf),
@@ -342,12 +357,11 @@
                 pltpu.SemaphoreType.DMA((2, 4)),
                 pltpu.SemaphoreType.DMA((SLOTS, 2, GROUPS)),
                 pltpu.SemaphoreType.DMA((n_chunks, 2, GROUPS)),
-                pltpu.SemaphoreType.DMA((n_chunks,)),
                 pltpu.SemaphoreType.REGULAR((2,)),
                 pltpu.SemaphoreType.REGULAR((2,)),
             ],
             compiler_params=pltpu.CompilerParams(
-                collective_id=0, has_side_effects=True, vmem_limit_bytes=67043328),
+                collective_id=0, has_side_effects=True, vmem_limit_bytes=50200000),
             name="stack",
         )(volume, filter_taps, mix_weights, mix_bias)
 

time: 392 us -> 395 us (level)
  the two profiles are of different devices: /device:TPU:122 before, /device:TPU:97 now
where the time goes in v3:
time: 395 us
  Pallas kernels  389 us (98%)
  local copies, waits for them, and re-layouts  6.16 us (2%)
    pallas_call x1, Pallas kernels, local_layers(): pl.pallas_call(functools.partial(stack_kernel, nx, ny), out_shape=pltpu.V...  389 us

profile of v3, /device:TPU:97, one launch (start us, length us, event | category | flops | bytes accessed | tf_op | source)
XLA Modules:
  0.0 395.0 jit_solution(8237394871581182015)
XLA Ops:
  0.0 388.8 %stack.1 = bf16[64,32,32,128]{3,2,1,0:T(8,128)(2,1)S(1)} custom-call(bf16[64,32,32,128]{3,2,1,0:T(8,128)(2,1)} %v_hbm.1, f32[3,3,21]{2,1,0:T(4,128)} %taps.1, bf16[3,64,64]{2,1,0:T(8,128)(2,1)} %weights.1, f32[3,64]{1,0:T(4,128)} %biases.1), custom_call_target="tpu_custom_call" | custom-call | tf_op jit(solution)/shard_map/stack/pallas_call | solution.py:340
  388.8 6.2 %copy.6 = bf16[64,32,32,128]{3,2,1,0:T(8,128)(2,1)} copy(bf16[64,32,32,128]{3,2,1,0:T(8,128)(2,1)S(1)} %stack.1) | data formatting | bytes 33554432

commit v4 on v3

--- a/solution.py
+++ b/solution.py
@@ -15,6 +15,7 @@
 CHUNK = 4
 GROUPS = 4
 SLOTS = 5
+X_UNROLL, Y_UNROLL = 8, 16
 
 
 def rows_cols(n_rows, n_cols):
@@ -83,9 +84,7 @@
     above = ((has_up, up), (has_down, down))
 
     def side_of(n):
-        m, b = n // 2, n % 2
-        swap = m * (middle - 1 - m) // 2
-        return b + swap - 2 * b * swap
+        return n % 2
 
     def chunk_of(n):
         return middle - 1 - n // 2 + side_of(n) * (1 + 2 * (n // 2))
@@ -168,18 +167,20 @@
             if turn == 0:
                 load(g).wait()
 
-            @pl.loop(0, per_group // 2)
+            @pl.loop(0, per_group // X_UNROLL)
             def _(p):
-                c = g * per_group + 2 * p
-                for t in range(2):
-                    pair = [vext[c + i, pl.ds(k * CHUNK, window), pl.ds(t * TILE, TILE)].reshape(window * TILE, depth)
-                            for i in range(2)]
-                    got = jnp.dot(ax[t], jnp.concatenate(pair, axis=1), preferred_element_type=jnp.float32)
-                    got = got.astype(jnp.bfloat16)
-                    for i in range(2):
-                        part = got[:, i * depth:(i + 1) * depth]
-                        u1[c + i, pl.ds(k * CHUNK, CHUNK), pl.ds(t * TILE, TILE)] = part[:own].reshape(CHUNK, TILE, depth)
-                        send[slot, t, c + i] = part[own:]
+                for h in range(X_UNROLL // 2):
+                    c = g * per_group + X_UNROLL * p + 2 * h
+                    for t in range(2):
+                        pair = [vext[c + i, pl.ds(k * CHUNK, window), pl.ds(t * TILE, TILE)].reshape(window * TILE, depth)
+                                for i in range(2)]
+                        got = jnp.dot(ax[t], jnp.concatenate(pair, axis=1), preferred_element_type=jnp.float32)
+                        got = got.astype(jnp.bfloat16)
+                        for i in range(2):
+                            part = got[:, i * depth:(i + 1) * depth]
+                            u1[c + i, pl.ds(k * CHUNK, CHUNK), pl.ds(t * TILE, TILE)] = part[:own].reshape(
+                                CHUNK, TILE, depth)
+                            send[slot, t, c + i] = part[own:]
 
             for s in range(2):
                 @pl.when(above[s][0])
@@ -202,10 +203,10 @@
                 def _():
                     y_copy(k, 0, s, g).wait_recv()
 
-            @pl.loop(0, per_group // 8)
+            @pl.loop(0, per_group // Y_UNROLL)
             def _(q):
-                for h in range(4):
-                    c = g * per_group + 8 * q + 2 * h
+                for h in range(Y_UNROLL // 2):
+                    c = g * per_group + Y_UNROLL * q + 2 * h
                     own = jnp.concatenate([u1[c + i, chunk].reshape(CHUNK * extent, depth) for i in range(2)], axis=1)
                     halo = jnp.concatenate([recv[k, c + i] for i in range(2)], axis=1)
                     rhs = jnp.concatenate([own, halo], axis=0)
@@ -279,17 +280,13 @@
                     recv[k, c, pl.ds(side * slab, slab)] = jnp.zeros((slab, depth), jnp.bfloat16)
 
     last = n_chunks - 1
-    early = 2
+    early = {n_chunks - 4: 0, n_chunks - 2: 1}
     for layer in range(n_layers):
-        for n in range(1, n_chunks - 2):
-            x_pass(layer, n)
-        set_other_matrices(layer)
-
-        @pl.loop(0, early)
-        def _(n):
-            yz_pass(layer, n)
-
-        for n in range(n_chunks - 2, n_chunks):
+        for n in range(1, n_chunks):
+            if n == 2:
+                set_other_matrices(layer)
+            if n in early:
+                yz_pass(layer, early[n])
             x_pass(layer, n)
         for side in range(2):
             @pl.when(beside[side][0])
@@ -301,7 +298,7 @@
 
         @pl.loop(0, last)
         def _(n):
-            @pl.when(n >= early)
+            @pl.when(n >= len(early))
             def _():
                 yz_pass(layer, n)
 

time: 395 us -> 356 us (0.901)
  the two profiles are of different devices: /device:TPU:97 before, /device:TPU:122 now
where the time goes in v4:
time: 356 us; the launch traced here: 354 us
  Pallas kernels  348 us (98%)
  local copies, waits for them, and re-layouts  6.16 us (2%)
    pallas_call x1, Pallas kernels, local_layers(): pl.pallas_call(functools.partial(stack_kernel, nx, ny), out_shape=pltpu.V...  348 us

profile of v4, /device:TPU:122, one launch (start us, length us, event | category | flops | bytes accessed | tf_op | source)
XLA Modules:
  0.0 354.0 jit_solution(4779438746610189235)
XLA Ops:
  0.0 347.9 %stack.1 = bf16[64,32,32,128]{3,2,1,0:T(8,128)(2,1)S(1)} custom-call(bf16[64,32,32,128]{3,2,1,0:T(8,128)(2,1)} %v_hbm.1, f32[3,3,21]{2,1,0:T(4,128)} %taps.1, bf16[3,64,64]{2,1,0:T(8,128)(2,1)} %weights.1, f32[3,64]{1,0:T(4,128)} %biases.1), custom_call_target="tpu_custom_call" | custom-call | tf_op jit(solution)/shard_map/stack/pallas_call | solution.py:337
  347.9 6.2 %copy.6 = bf16[64,32,32,128]{3,2,1,0:T(8,128)(2,1)} copy(bf16[64,32,32,128]{3,2,1,0:T(8,128)(2,1)S(1)} %stack.1) | data formatting | bytes 33554432
